TPU v7x, 256 devices: a whole 4x4x8 slice. The times are simulated.
256 devices in a mesh: row: 8 (over y, core), col: 4 (over x), layer: 8 (over z).
Axes of the slice: x: 4, y: 4, z: 8, core: 2. Of those that a mesh axis runs over, the one named last changes fastest.
Arguments:
- hamiltonian: bfloat16 [5120, 5120], P(('row', 'layer'), 'col'), may hold values from -1.2 to 1.2, as said below
- tile_pattern: int32 [40, 40], replicated, may hold values from 0 to 1, as said below
- n_occ: int32 [1], replicated, may hold values from 1024 to 4095
- mu: float32 [1], replicated, may hold values from -0.2 to 0.2
- gamma: float32 [1], replicated, may hold values from 0.25 to 0.4
Outputs:
- density: float32 [5120, 5120], P(('row', 'layer'), 'col')
Inputs may be any that keep to these rules, and one draw needn't show every extreme that they name: `tile_pattern`: Symmetric, 0 or 1, with ones on the diagonal and next to it. `hamiltonian`: Symmetric; its eigenvalues lie within -1.8 and 1.8.
All inputs are finite; a program needn't handle non-finite values.
Results may differ from a plain program's by a relative error of at most 0.0055.
Values may be sent and summed in bfloat16 or wider, within the bound.
A program may use at most 64 MiB of HBM per device.

v0:
```python
import jax
import jax.numpy as jnp
from jax import lax
from jax.sharding import PartitionSpec as P

TILE = 128
STEPS = 2


def element_mask(tile_pattern, row_start, row_count, col_start, col_count):
    tile_count = tile_pattern.shape[0]
    tile_ids = jnp.arange(tile_count, dtype=jnp.int32)
    row_tiles = (row_start + jnp.arange(row_count, dtype=jnp.int32)) // TILE
    col_tiles = (col_start + jnp.arange(col_count, dtype=jnp.int32)) // TILE
    row_hot = (row_tiles[:, None] == tile_ids[None, :]).astype(jnp.bfloat16)
    col_hot = (tile_ids[:, None] == col_tiles[None, :]).astype(jnp.bfloat16)
    picked = jnp.dot(row_hot, tile_pattern.astype(jnp.bfloat16), preferred_element_type=jnp.float32)
    return jnp.dot(picked.astype(jnp.bfloat16), col_hot, preferred_element_type=jnp.float32)


def shards(hamiltonian, tile_pattern, n_occ, mu, gamma):
    share_rows, band_cols = hamiltonian.shape
    n_col = lax.axis_size("col")
    n_layer = lax.axis_size("layer")
    order = band_cols * n_col
    layer_index = lax.axis_index("layer")
    row_start = (lax.axis_index("row") * n_layer + layer_index) * share_rows
    col_start = lax.axis_index("col") * band_cols
    mask = element_mask(tile_pattern, row_start, share_rows, col_start, band_cols)
    row_global = row_start + jnp.arange(share_rows, dtype=jnp.int32)
    col_global = col_start + jnp.arange(band_cols, dtype=jnp.int32)
    identity = (row_global[:, None] == col_global[None, :]).astype(jnp.float32)
    filling = n_occ[0].astype(jnp.float32) / order
    start = mask * (
        filling * identity + gamma[0] * (mu[0] * identity - hamiltonian.astype(jnp.float32))
    )
    current = start.astype(jnp.bfloat16)
    result = start
    for iteration in range(STEPS):
        column = lax.all_gather(current, ("row", "layer"), axis=0, tiled=True)

        def rows_product(left_share):
            return jnp.dot(
                lax.all_gather(left_share, "col", axis=1, tiled=True),
                column,
                preferred_element_type=jnp.float32,
            )

        square = mask * rows_product(current)
        cube = mask * rows_product(square.astype(jnp.bfloat16))
        result = 3.0 * square - 2.0 * cube
        current = result.astype(jnp.bfloat16)
    return result


def solution(mesh):
    placed = (P(("row", "layer"), "col"), P(), P(), P(), P())
    return jax.shard_map(
        shards, mesh=mesh, in_specs=placed, out_specs=P(("row", "layer"), "col"), check_vma=False
    )
```

profile of v0, /device:TPU:1, one launch (start us, length us, event | category | flops | bytes accessed | tf_op | source)
XLA Modules:
  0.0 247.4 jit_solution(11599922052640103232)
XLA Ops:
  6.5 0.0 all-gather.3.cloned.1.call-start
  8.5 2.0 fusion.8
  10.5 0.0 all-gather.3.cloned.1.call-update
  10.6 0.0 all-gather.5.cloned.1.call-start
  10.6 13.2 %all_gather.18 = bf16[80,5120]{1,0:T(8,128)(2,1)S(1)} all-gather(bf16[80,1280]{1,0:T(8,128)(2,1)} %get-tuple-element.5), channel_id=1, replica_groups=mesh['row'=8,'col'=4,'layer'=8] {'col'}, dimensions={1}, use_global_device_ids=true | all-gather | bytes 1024000 | tf_op jit(solution)/shard_map/all_gather | solution.py:44
  23.8 81.8 %all-gather.3.cloned.1.call-done = bf16[5120,1280]{1,0:T(8,128)(2,1)} async-done(((bf16[80,1280]{1,0:T(8,128)(2,1)}), bf16[5120,1280]{1,0:T(8,128)(2,1)}) %all-gather.3.cloned.1.call-update) | async-done | bytes 13107216 | tf_op jit(solution)/shard_map/all_gather | solution.py:40
  105.6 0.0 copy-start
  105.6 7.2 %fusion.21 = (bf16[80,1280]{1,0:T(8,128)(2,1)S(1)}, f32[80,1280]{1,0:T(8,128)S(1)}) fusion(f32[80,1280]{1,0:T(8,128)S(1)} %get-tuple-element.6, bf16[80,5120]{1,0:T(8,128)(2,1)S(1)} %all_gather.18, bf16[5120,1280]{1,0:T(8,128)(2,1)} %all-gather.3.cloned.1.call-done), kind=kOutput, calls=%fused_computation.37 | convolution fusion | flops 1048780800 | bytes 14950400 | tf_op jit(solution)/shard_map/dot_general | solution.py:43
  112.8 12.2 %all_gather.20 = bf16[80,5120]{1,0:T(8,128)(2,1)S(1)} all-gather(bf16[80,1280]{1,0:T(8,128)(2,1)S(1)} %get-tuple-element.7), channel_id=1, replica_groups=mesh['row'=8,'col'=4,'layer'=8] {'col'}, dimensions={1}, use_global_device_ids=true | all-gather | bytes 1024000 | tf_op jit(solution)/shard_map/all_gather | solution.py:44
  125.0 0.0 copy-done
  125.0 3.1 %fusion.4 = bf16[80,1280]{1,0:T(8,128)(2,1)} fusion(f32[80,1280]{1,0:T(8,128)S(1)} %get-tuple-element.6, bf16[80,5120]{1,0:T(8,128)(2,1)S(1)} %all_gather.20, bf16[5120,1280]{1,0:T(8,128)(2,1)S(1)} %copy-done, f32[80,1280]{1,0:T(8,128)S(1)} %get-tuple-element.8), kind=kOutput, calls=%fused_computation.8 | convolution fusion | flops 1049088000 | bytes 14950400 | tf_op jit(solution)/shard_map/dot_general | solution.py:43
  128.1 0.0 all-gather.5.cloned.1.call-update
  128.1 10.8 %all_gather.21 = bf16[80,5120]{1,0:T(8,128)(2,1)S(1)} all-gather(bf16[80,1280]{1,0:T(8,128)(2,1)} %fusion.4), channel_id=1, replica_groups=mesh['row'=8,'col'=4,'layer'=8] {'col'}, dimensions={1}, use_global_device_ids=true | all-gather | bytes 1024000 | tf_op jit(solution)/shard_map/all_gather | solution.py:44
  138.9 79.2 %all-gather.5.cloned.1.call-done = bf16[5120,1280]{1,0:T(8,128)(2,1)} async-done(((bf16[80,1280]{1,0:T(8,128)(2,1)}), bf16[5120,1280]{1,0:T(8,128)(2,1)}) %all-gather.5.cloned.1.call-update) | async-done | bytes 13107216 | tf_op jit(solution)/shard_map/all_gather | solution.py:40
  218.0 0.0 copy-start.1
  218.0 7.2 %fusion.22 = (bf16[80,1280]{1,0:T(8,128)(2,1)S(1)}, f32[80,1280]{1,0:T(8,128)S(1)}) fusion(f32[80,1280]{1,0:T(8,128)S(1)} %get-tuple-element.6, bf16[80,5120]{1,0:T(8,128)(2,1)S(1)} %all_gather.21, bf16[5120,1280]{1,0:T(8,128)(2,1)} %all-gather.5.cloned.1.call-done), kind=kOutput, calls=%fused_computation.38 | convolution fusion | flops 1048780800 | bytes 14950400 | tf_op jit(solution)/shard_map/dot_general | solution.py:43
  225.3 12.2 %all_gather.23 = bf16[80,5120]{1,0:T(8,128)(2,1)S(1)} all-gather(bf16[80,1280]{1,0:T(8,128)(2,1)S(1)} %get-tuple-element.9), channel_id=1, replica_groups=mesh['row'=8,'col'=4,'layer'=8] {'col'}, dimensions={1}, use_global_device_ids=true | all-gather | bytes 1024000 | tf_op jit(solution)/shard_map/all_gather | solution.py:44
  237.4 0.0 copy-done.1
  237.5 3.1 %fusion.2 = f32[80,1280]{1,0:T(8,128)} fusion(f32[80,1280]{1,0:T(8,128)S(1)} %get-tuple-element.6, bf16[80,5120]{1,0:T(8,128)(2,1)S(1)} %all_gather.23, bf16[5120,1280]{1,0:T(8,128)(2,1)S(1)} %copy-done.1, f32[80,1280]{1,0:T(8,128)S(1)} %get-tuple-element.10), kind=kOutput, calls=%fused_computation.6 | convolution fusion | flops 1048985600 | bytes 15155200 | tf_op jit(solution)/shard_map/dot_general | solution.py:43
  (2 shorter events, 0.0 us)
Async XLA Ops:
  6.5 99.0 %all-gather.3.cloned.1.call-start = ((), (), s32[]{:S(2)}) async-start(), calls=%async_computation | async-start | bytes 13312000 | tf_op jit(solution)/shard_map/all_gather | solution.py:40
  10.6 207.4 %all-gather.5.cloned.1.call-start = ((), (), s32[]{:S(2)}) async-start(), calls=%async_computation.1 | async-start | bytes 13312000 | tf_op jit(solution)/shard_map/all_gather | solution.py:40
  105.6 19.4 %copy-start = (bf16[5120,1280]{1,0:T(8,128)(2,1)S(1)}, bf16[5120,1280]{1,0:T(8,128)(2,1)}, u32[]{:S(2)}) copy-start(bf16[5120,1280]{1,0:T(8,128)(2,1)} %all-gather.3.cloned.1.call-done) | copy-start | bytes 39321604
  218.0 19.4 %copy-start.1 = (bf16[5120,1280]{1,0:T(8,128)(2,1)S(1)}, bf16[5120,1280]{1,0:T(8,128)(2,1)}, u32[]{:S(2)}) copy-start(bf16[5120,1280]{1,0:T(8,128)(2,1)} %all-gather.5.cloned.1.call-done) | copy-start | bytes 39321604
Sparse Core Ops, SparseCore 0:
  10.7 94.8 all-gather.2
  128.2 89.7 all-gather.4
where the time goes:
time: 249 us; the launch traced here: 247 us
  waiting for transfers between devices  161 us (65%)
  blocking collectives  48.3 us (19%)
  matrix products  22.7 us (9%)
  between operations  15.4 us (6%)
    all_gather x2, waiting for transfers between devices, shards(): column = lax.all_gather(current, ('row', 'layer'), axis=0, tiled=True)  161 us
    all_gather x4, blocking collectives, rows_product(): lax.all_gather(left_share, 'col', axis=1, tiled=True)  48.3 us
    dot_general x4, matrix products, rows_product(): jnp.dot(lax.all_gather(left_share, 'col', axis=1, tiled=True), column, pr...  20.7 us
  transfers between devices with their start and end apart: 2, of which 2 were waited for; matrix products, arithmetic and copies ran while one was open for 0% of the time, Pallas kernels for 0%

commit v1 on v0

v1 whole, which is shorter than its diff:
```python
import functools
import heapq

import jax
import jax.numpy as jnp
from jax import lax
from jax.experimental import pallas as pl
from jax.experimental.pallas import tpu as pltpu
from jax.sharding import PartitionSpec as P

TILE = 128
LANES = 128
STEPS = 2
MESH = pl.DeviceIdType.MESH
CHUNK = 256


def gather_schedule(ny, nz, rows, cols, first_cols, rate=46.65, lat=1.9):
    ring = {"y": ny, "z": nz}
    free, events, ops, count = {}, [], [], 0

    def send(t, axis, sign, piece, hops):
        nonlocal count
        h, dy, dz, c0, w = piece
        begin = max(t, free.get((axis, sign), 0.0))
        end = begin + rows * w * 2 / rate / 1000
        free[axis, sign] = end
        landed = (h, dy - sign, dz, c0, w) if axis == "y" else (h, dy, dz - sign, c0, w)
        heapq.heappush(events, (end + lat, count, axis, sign, landed, hops + 1))
        ops.append(("send", axis, sign, piece, count))
        count += 1

    def forward(t, axis, sign, piece, hops):
        h, dy, dz, c0, w = piece
        half = ring[axis] // 2
        if hops < half - 1:
            send(t, axis, sign, piece, hops)
        elif hops == half - 1:
            part = (w // 2 + (0 if c0 <= first_cols else LANES - 1)) // LANES * LANES
            send(t, axis, sign, (h, dy, dz, c0, part) if sign > 0 else (h, dy, dz, c0 + part, w - part), hops)

    own = {1: (1, 0, 0, 0, first_cols), 2: (2, 0, 0, first_cols, cols - first_cols)}
    for turn in (0, 1):
        for sign in (1, -1):
            send(0.0, "y", sign, own[1 + turn], 0)
            send(0.0, "z", sign, own[2 - turn], 0)
    while events:
        t, receive, axis, sign, piece, hops = heapq.heappop(events)
        ops.append(("wait", piece, receive))
        forward(t, axis, sign, piece, hops)
        if axis == ("y" if piece[0] == 1 else "z"):
            for way in (1, -1):
                send(t, "z" if axis == "y" else "y", way, piece, 0)
    return ops, count


def kernel(sizes, ops, h_ref, pattern_ref, occ_ref, mu_ref, gamma_ref, out_ref,
           band, left, mask, square, total, current, band_recv, band_send, pair_sem, left_recv, left_send):
    nx, ny, nz, rows, cols = sizes
    order = nx * cols
    half = ny * nz * rows
    row, x, z = lax.axis_index("row"), lax.axis_index("col"), lax.axis_index("layer")
    y, core = row // 2, row % 2
    partner = {"row": 2 * y + 1 - core}

    def there(axis, sign):
        if axis == "y":
            return {"row": 2 * ((y + sign + ny) % ny) + core}
        if axis == "z":
            return {"layer": (z + sign + nz) % nz}
        return {"col": (x + sign + nx) % nx}

    row0 = pl.multiple_of((row * nz + z) * rows, 16)
    col0 = pl.multiple_of(x * cols, 128)

    barrier = pltpu.get_barrier_semaphore()
    friends = [partner] + [there(a, g) for a in ("x", "y", "z") for g in (1, -1)]
    for friend in friends:
        pl.semaphore_signal(barrier, inc=1, device_id=friend, device_id_type=MESH)

    tiles = pattern_ref.shape[0]
    row_tile = (row0 + lax.broadcasted_iota(jnp.int32, (rows, tiles), 0)) // TILE
    row_hot = (row_tile == lax.broadcasted_iota(jnp.int32, (rows, tiles), 1)).astype(jnp.bfloat16)
    col_tile = (col0 + lax.broadcasted_iota(jnp.int32, (tiles, cols), 1)) // TILE
    col_hot = (col_tile == lax.broadcasted_iota(jnp.int32, (tiles, cols), 0)).astype(jnp.bfloat16)
    picked = jnp.dot(row_hot, pattern_ref[...].astype(jnp.float32).astype(jnp.bfloat16),
                     preferred_element_type=jnp.float32)
    mask[...] = jnp.dot(picked.astype(jnp.bfloat16), col_hot, preferred_element_type=jnp.float32)
    identity = (row0 + lax.broadcasted_iota(jnp.int32, (rows, cols), 0)
                == col0 + lax.broadcasted_iota(jnp.int32, (rows, cols), 1)).astype(jnp.float32)
    filling = occ_ref[0].astype(jnp.float32) / order
    start = mask[...] * (filling * identity + gamma_ref[0] * (mu_ref[0] * identity - h_ref[...].astype(jnp.float32)))
    current[...] = start.astype(jnp.bfloat16)

    pl.semaphore_wait(barrier, len(friends))

    def step(s, carry):
        def block(piece):
            _, dy, dz, c0, w = piece
            origin = (2 * ((y + dy + ny) % ny) + core) * nz + (z + dz + nz) % nz
            return band.at[s, pl.ds(pl.multiple_of(origin * rows, 16), rows), pl.ds(c0, w)]

        def to_partner(ref):
            return pltpu.make_async_remote_copy(
                src_ref=ref, dst_ref=ref, send_sem=pair_sem.at[s, 0], recv_sem=pair_sem.at[s, 1],
                device_id=partner, device_id_type=MESH)

        def along(axis, sign, piece, receive):
            ref = block(piece)
            return pltpu.make_async_remote_copy(
                src_ref=ref, dst_ref=ref, send_sem=band_send.at[s], recv_sem=band_recv.at[s, receive],
                device_id=there(axis, sign), device_id_type=MESH)

        def left_block(which, dx, c0, w):
            at = pl.multiple_of(((x + dx + nx) % nx) * cols + c0, 128)
            return left.at[s, which, :, pl.ds(at, w)]

        def left_copy(which, sign, dx, c0, w, receive):
            ref = left_block(which, dx, c0, w)
            return pltpu.make_async_remote_copy(
                src_ref=ref, dst_ref=ref, send_sem=left_send.at[s, which], recv_sem=left_recv.at[s, which, receive],
                device_id=there("x", sign), device_id_type=MESH)

        band[s, pl.ds(row0, rows), :] = current[...]
        left[s, 0, :, pl.ds(col0, cols)] = current[...]

        mid = cols // 2
        left_copy(0, 1, 0, 0, cols, 0).start()
        left_copy(0, -1, 0, 0, cols, 1).start()

        told, forwarded = False, False
        for op in ops:
            if op[0] == "send":
                along(*op[1:]).start()
                continue
            if not told:
                told = True
                to_partner(band.at[s, pl.ds(row0, rows), :]).start()
            _, piece, receive = op
            along("y", 1, piece, receive).wait_recv()
            to_partner(block(piece)).start()
            if not forwarded and receive > 12:
                forwarded = True
                left_copy(0, 1, -1, 0, cols, 0).wait_recv()
                left_copy(0, 1, -1, 0, mid, 2).start()
                left_copy(0, -1, 1, 0, cols, 1).wait_recv()
                left_copy(0, -1, 1, mid, mid, 3).start()
        left_copy(0, 1, -2, 0, mid, 2).wait_recv()
        left_copy(0, -1, -2, mid, mid, 3).wait_recv()
        everything = band.at[s, pl.ds(0, half), :]
        pltpu.make_async_copy(everything, everything, pair_sem.at[s, 1]).wait()

        def chunk_parts(c0):
            ways = []
            if c0 < mid:
                ways.append((1, c0, min(CHUNK, mid - c0)))
            if c0 + CHUNK > mid:
                begin = max(c0, mid)
                ways.append((-1, begin, c0 + CHUNK - begin))
            return ways

        n_chunks = cols // CHUNK
        walk = sorted(range(n_chunks), key=lambda n: min(n, n_chunks - 1 - n))
        for n in walk:
            c0 = n * CHUNK
            product = jnp.dot(left[s, 0], band[s, :, c0:c0 + CHUNK], preferred_element_type=jnp.float32)
            product = mask[:, c0:c0 + CHUNK] * product
            square[:, c0:c0 + CHUNK] = product
            left[s, 1, :, pl.ds(pl.multiple_of(col0 + c0, 128), CHUNK)] = product.astype(jnp.bfloat16)
            for way, sign in enumerate((1, -1)):
                left_copy(1, sign, 0, c0, CHUNK, 2 * n + way).start()
        far = {}
        for n in walk:
            c0 = n * CHUNK
            for way, sign in enumerate((1, -1)):
                left_copy(1, sign, -sign, c0, CHUNK, 2 * n + way).wait_recv()
                for go, begin, width in chunk_parts(c0):
                    if go == sign:
                        far[begin] = (sign, begin, width, 2 * n_chunks + len(far))
                        left_copy(1, sign, -sign, begin, width, far[begin][3]).start()

        def add(dx, first):
            at = pl.multiple_of(((x + dx + nx) % nx) * cols, 128)
            for n in range(n_chunks):
                c0 = n * CHUNK
                part = jnp.dot(left[s, 1, :, pl.ds(at, cols)], band[s, pl.ds(at, cols), c0:c0 + CHUNK],
                               preferred_element_type=jnp.float32)
                if first:
                    total[:, c0:c0 + CHUNK] = part
                else:
                    total[:, c0:c0 + CHUNK] += part

        add(0, True)
        add(-1, False)
        add(1, False)
        for sign, begin, width, receive in far.values():
            left_copy(1, sign, -2, begin, width, receive).wait_recv()
        add(2, False)
        result = 3.0 * square[...] - 2.0 * (mask[...] * total[...])
        out_ref[...] = result
        current[...] = result.astype(jnp.bfloat16)

        sent = band.at[s, pl.ds(0, half - rows), :]
        pltpu.make_async_copy(sent, sent, band_send.at[s]).wait()
        pltpu.make_async_copy(everything, everything, pair_sem.at[s, 0]).wait()
        for which in (0, 1):
            ref = left.at[s, which, :, pl.ds(0, 3 * cols)]
            pltpu.make_async_copy(ref, ref, left_send.at[s, which]).wait()
        return carry

    lax.fori_loop(0, STEPS, step, 0)


def solution(mesh):
    nx, ny, nz = mesh.shape["col"], mesh.shape["row"] // 2, mesh.shape["layer"]

    def shards(hamiltonian, tile_pattern, n_occ, mu, gamma):
        rows, cols = hamiltonian.shape
        order = nx * cols
        ops, count = gather_schedule(ny, nz, rows, cols, 512)
        vmem = pl.BlockSpec(memory_space=pltpu.VMEM)
        smem = pl.BlockSpec(memory_space=pltpu.SMEM)
        return pl.pallas_call(
            functools.partial(kernel, (nx, ny, nz, rows, cols), ops),
            out_shape=jax.ShapeDtypeStruct((rows, cols), jnp.float32),
            in_specs=[vmem, vmem, smem, smem, smem],
            out_specs=vmem,
            scratch_shapes=[
                pltpu.VMEM((STEPS, order, cols), jnp.bfloat16),
                pltpu.VMEM((STEPS, 2, rows, order), jnp.bfloat16),
                pltpu.VMEM((rows, cols), jnp.float32),
                pltpu.VMEM((rows, cols), jnp.float32),
                pltpu.VMEM((rows, cols), jnp.float32),
                pltpu.VMEM((rows, cols), jnp.bfloat16),
                pltpu.SemaphoreType.DMA((STEPS, count)),
                pltpu.SemaphoreType.DMA((STEPS,)),
                pltpu.SemaphoreType.DMA((STEPS, 2)),
                pltpu.SemaphoreType.DMA((STEPS, 2, 16)),
                pltpu.SemaphoreType.DMA((STEPS, 2)),
            ],
            compiler_params=pltpu.CompilerParams(
                collective_id=0, has_side_effects=True, vmem_limit_bytes=48 * 2**20),
            name="purify",
        )(hamiltonian, tile_pattern, n_occ, mu, gamma)

    placed = (P(("row", "layer"), "col"), P(), P(), P(), P())
    return jax.shard_map(
        shards, mesh=mesh, in_specs=placed, out_specs=P(("row", "layer"), "col"), check_vma=False
    )
```

time: 249 us -> 121 us (0.49)
  waiting for transfers between devices: 161 us -> 0 us
  Pallas kernels: 0 us -> 116 us
  blocking collectives: 48.3 us -> 0 us
  matrix products: 22.7 us -> 0 us
  between operations: 15.4 us -> 1.96 us
    all_gather x2 -> x0, waiting for transfers between devices: 161 us -> none  [shards(): column = lax.all_gather(current, ('row', 'layer'), axis=0, tiled=True)]
    pallas_call x0 -> x1, Pallas kernels: none -> 116 us  [shards(): pl.pallas_call(functools.partial(kernel, (nx, ny, nz, rows, cols), ops),...]
    all_gather x4 -> x0, blocking collectives: 48.3 us -> none  [rows_product(): lax.all_gather(left_share, 'col', axis=1, tiled=True)]
    dot_general x5 -> x0, matrix products: 22.7 us -> none  [the longest x4 20.7 us: rows_product(): jnp.dot(lax.all_gather(left_share, 'col', axis=1, tiled=True), column, pr...]
  transfers between devices with their start and end apart: 2 -> 0, of which waited for: 2 -> 0; matrix products, arithmetic and copies ran while one was open for 0% -> 0% of each run, Pallas kernels for 0% -> 0%
where the time goes in v1:
time: 121 us
  Pallas kernels  116 us (96%)
  local copies, waits for them, and re-layouts  2.4 us (2%)
  between operations  1.96 us (2%)
    pallas_call x1, Pallas kernels, shards(): pl.pallas_call(functools.partial(kernel, (nx, ny, nz, rows, cols), ops),...  116 us

profile of v1, /device:TPU:1, one launch (start us, length us, event | category | flops | bytes accessed | tf_op | source)
XLA Modules:
  0.0 120.8 jit_solution(1068186624086219873)
XLA Ops:
  1.9 0.0 copy-start
  2.0 0.9 copy-done
  2.9 0.0 copy-start.1
  2.9 0.7 copy-done.1
  3.6 116.4 %purify.1 = f32[80,1280]{1,0:T(8,128)S(1)} custom-call(bf16[80,1280]{1,0:T(8,128)(2,1)S(1)} %copy-done, s32[40,40]{1,0:T(8,128)S(1)} %copy-done.1, s32[1]{0:T(128)S(6)} %copy.7.occ_ref, f32[1]{0:T(128)S(6)} %copy.8.mu_ref, f32[1]{0:T(128)S(6)} %copy.9.gamma_ref), custom_call_target="tpu_custom_call" | custom-call | tf_op jit(solution)/shard_map/purify/pallas_call | solution.py:223
  120.0 0.8 copy.10
Async XLA Ops:
  1.9 0.9 copy-start
  2.9 0.7 copy-start.1

commit v2 on v1

v2 whole, which is shorter than its diff:
```python
import functools
import heapq

import jax
import jax.numpy as jnp
from jax import lax
from jax.experimental import pallas as pl
from jax.experimental.pallas import tpu as pltpu
from jax.sharding import PartitionSpec as P

TILE = 128
LANES = 128
STEPS = 2
MESH = pl.DeviceIdType.MESH
CHUNK = 256
CHUNKS = ((0, "y"), (1, "z"), (3, "y"), (2, "z"), (4, "z"))


def gather_schedule(ny, nz, rows, chunks, rate=46.65, lat=1.9, ahead=0.8, partner=1.5, late=3.1, product=0.7, hop=3.0):
    ring = {"y": ny, "z": nz}
    free, events, ops, waiting = {}, [], [], {}
    missing = {(n, dy): (nz - (dy == 0)) * c[1] for n, c in enumerate(chunks) for dy in range(ny)}
    blocks = [0] * len(chunks)
    count = 0

    def later(t, *event):
        heapq.heappush(events, (t, len(ops), len(events), *event))

    def offer(axis, sign, piece, hops):
        n, dy, dz, c0, w = piece
        half = ring[axis] // 2
        if hops == half:
            return
        if hops == half - 1:
            if w > LANES:
                cut = w // 2 // LANES * LANES
                piece = (n, dy, dz, c0, cut) if sign > 0 else (n, dy, dz, c0 + cut, w - cut)
            elif (sign > 0) != (c0 // LANES % 2 == 0):
                return
        second = axis != chunks[n][2]
        waiting.setdefault((axis, sign), []).append(((n + late * second, second, hops), piece, hops))

    def pump(t):
        nonlocal count
        for (axis, sign), queue in waiting.items():
            while queue and free.get((axis, sign), 0.0) - ahead <= t:
                queue.sort(key=lambda entry: entry[0])
                _, piece, hops = queue.pop(0)
                n, dy, dz, c0, w = piece
                end = max(t, free.get((axis, sign), 0.0)) + rows * w * 2 / rate / 1000
                free[axis, sign] = end
                ops.append(("send", axis, sign, piece, count))
                landed = (n, dy - sign, dz, c0, w) if axis == "y" else (n, dy, dz - sign, c0, w)
                later(end + lat, "land", axis, sign, landed, hops + 1, count)
                later(end - ahead, "free")
                count += 1

    for n, (c0, w, _) in enumerate(chunks):
        for axis in "yz":
            for sign in (1, -1):
                offer(axis, sign, (n, 0, 0, c0, w), 0)
    pump(0.0)
    while events:
        t, _, _, kind, *rest = heapq.heappop(events)
        if kind == "land":
            axis, sign, piece, hops, receive = rest
            n, dy, dz, c0, w = piece
            ops.append(("wait", piece, receive))
            offer(axis, sign, piece, hops)
            if axis == chunks[n][2]:
                for way in (1, -1):
                    offer("z" if axis == "y" else "y", way, piece, 0)
            missing[n, dy % ny] -= w
            if missing[n, dy % ny] == 0:
                ops.append(("pair", n, dy % ny))
                blocks[n] += 1
                if blocks[n] == ny:
                    later(t + partner, "square", n)
        elif kind == "square":
            ops.append(("square", rest[0]))
            later(t + product + hop, "relay", rest[0])
        elif kind == "relay":
            ops.append(("relay", rest[0]))
        pump(t)
    return ops, count


def kernel(sizes, chunks, ops, h_ref, pattern_ref, occ_ref, mu_ref, gamma_ref, out_ref,
           band, left, mask, square, total, current, band_recv, band_send, pair_recv, pair_send, left_recv, left_send):
    nx, ny, nz, rows, cols = sizes
    order = nx * cols
    half = ny * nz * rows
    row, x, z = lax.axis_index("row"), lax.axis_index("col"), lax.axis_index("layer")
    y, core = row // 2, row % 2
    partner = {"row": 2 * y + 1 - core}
    to = {}
    for sign in (1, -1):
        to["x", sign] = {"col": (x + sign + nx) % nx}
        to["y", sign] = {"row": 2 * ((y + sign + ny) % ny) + core}
        to["z", sign] = {"layer": (z + sign + nz) % nz}
    row0 = pl.multiple_of((row * nz + z) * rows, 16)
    col0 = pl.multiple_of(x * cols, 128)

    barrier = pltpu.get_barrier_semaphore()
    friends = [partner, *to.values()]
    for friend in friends:
        pl.semaphore_signal(barrier, inc=1, device_id=friend, device_id_type=MESH)

    tiles = pattern_ref.shape[0]
    row_tile = (row0 + lax.broadcasted_iota(jnp.int32, (rows, tiles), 0)) // TILE
    row_hot = (row_tile == lax.broadcasted_iota(jnp.int32, (rows, tiles), 1)).astype(jnp.bfloat16)
    col_tile = (col0 + lax.broadcasted_iota(jnp.int32, (tiles, cols), 1)) // TILE
    col_hot = (col_tile == lax.broadcasted_iota(jnp.int32, (tiles, cols), 0)).astype(jnp.bfloat16)
    picked = jnp.dot(row_hot, pattern_ref[...].astype(jnp.float32).astype(jnp.bfloat16),
                     preferred_element_type=jnp.float32)
    mask[...] = jnp.dot(picked.astype(jnp.bfloat16), col_hot, preferred_element_type=jnp.float32)
    identity = (row0 + lax.broadcasted_iota(jnp.int32, (rows, cols), 0)
                == col0 + lax.broadcasted_iota(jnp.int32, (rows, cols), 1)).astype(jnp.float32)
    filling = occ_ref[0].astype(jnp.float32) / order
    start = mask[...] * (filling * identity + gamma_ref[0] * (mu_ref[0] * identity - h_ref[...].astype(jnp.float32)))
    current[...] = start.astype(jnp.bfloat16)

    pl.semaphore_wait(barrier, len(friends))

    def step(s, carry):
        def along(axis, sign, piece, receive):
            _, dy, dz, c0, w = piece
            origin = (2 * ((y + dy + ny) % ny) + core) * nz + (z + dz + nz) % nz
            ref = band.at[s, pl.ds(pl.multiple_of(origin * rows, 16), rows), pl.ds(c0, w)]
            return pltpu.make_async_remote_copy(
                src_ref=ref, dst_ref=ref, send_sem=band_send.at[s], recv_sem=band_recv.at[s, receive],
                device_id=to[axis, sign], device_id_type=MESH)

        def to_partner(n, dy):
            begin = pl.multiple_of((2 * ((y + dy) % ny) + core) * nz * rows, 16)
            ref = band.at[s, pl.ds(begin, nz * rows), pl.ds(*chunks[n][:2])]
            return pltpu.make_async_remote_copy(
                src_ref=ref, dst_ref=ref, send_sem=pair_send.at[s], recv_sem=pair_recv.at[s, n],
                device_id=partner, device_id_type=MESH)

        def along_x(which, sign, dx, c0, w, receive):
            at = pl.multiple_of(((x + dx + nx) % nx) * cols + c0, 128)
            ref = left.at[s, which, :, pl.ds(at, w)]
            return pltpu.make_async_remote_copy(
                src_ref=ref, dst_ref=ref, send_sem=left_send.at[s, which], recv_sem=left_recv.at[s, which, receive],
                device_id=to["x", sign], device_id_type=MESH)

        band[s, pl.ds(row0, rows), :] = current[...]
        left[s, 0, :, pl.ds(col0, cols)] = current[...]

        mid = cols // 2

        def left_begin():
            along_x(0, 1, 0, 0, cols, 0).start()
            along_x(0, -1, 0, 0, cols, 1).start()

        def left_relay():
            along_x(0, 1, -1, 0, cols, 0).wait_recv()
            along_x(0, 1, -1, 0, mid, 2).start()
            along_x(0, -1, 1, 0, cols, 1).wait_recv()
            along_x(0, -1, 1, mid, mid, 3).start()

        def left_end():
            along_x(0, 1, -2, 0, mid, 2).wait_recv()
            along_x(0, -1, -2, mid, mid, 3).wait_recv()

        def square_chunk(n):
            c0, w, _ = chunks[n]
            arrived = band.at[s, pl.ds(0, half), pl.ds(c0, w)]
            pltpu.make_async_copy(arrived, arrived, pair_recv.at[s, n]).wait()
            product = jnp.dot(left[s, 0], band[s, :, c0:c0 + w], preferred_element_type=jnp.float32)
            product = mask[:, c0:c0 + w] * product
            square[:, c0:c0 + w] = product
            left[s, 1, :, pl.ds(pl.multiple_of(col0 + c0, 128), w)] = product.astype(jnp.bfloat16)
            along_x(1, 1, 0, c0, w, 4 * n).start()
            along_x(1, -1, 0, c0, w, 4 * n + 1).start()

        def relay_chunk(n):
            c0, w, _ = chunks[n]
            cut = w // 2
            along_x(1, 1, -1, c0, w, 4 * n).wait_recv()
            along_x(1, 1, -1, c0, cut, 4 * n + 2).start()
            along_x(1, -1, 1, c0, w, 4 * n + 1).wait_recv()
            along_x(1, -1, 1, c0 + cut, w - cut, 4 * n + 3).start()

        def far_chunk(n):
            c0, w, _ = chunks[n]
            cut = w // 2
            along_x(1, 1, -2, c0, cut, 4 * n + 2).wait_recv()
            along_x(1, -1, -2, c0 + cut, w - cut, 4 * n + 3).wait_recv()

        def cube_part(dx, k0, width, first=False):
            at = pl.multiple_of(((x + dx + nx) % nx) * cols + k0, 128)
            for c0, w, _ in chunks:
                part = jnp.dot(left[s, 1, :, pl.ds(at, width)], band[s, pl.ds(at, width), c0:c0 + w],
                               preferred_element_type=jnp.float32)
                if first:
                    total[:, c0:c0 + w] = part
                else:
                    total[:, c0:c0 + w] += part

        begun, relayed, squared, passed = False, False, [], []
        for op in ops:
            if op[0] == "send":
                along(*op[1:]).start()
            elif op[0] == "wait":
                if not begun:
                    begun = True
                    left_begin()
                along("y", 1, *op[1:]).wait_recv()
                if not relayed and op[2] > 40:
                    relayed = True
                    left_relay()
            elif op[0] == "pair":
                to_partner(*op[1:]).start()
            elif op[0] == "square":
                if not squared:
                    left_end()
                square_chunk(op[1])
                squared.append(op[1])
            elif len(squared) < len(chunks):
                relay_chunk(op[1])
                passed.append(op[1])
        for n in passed:
            far_chunk(n)
        rest = [n for n in squared if n not in passed]
        known = min(chunks[n][0] for n in rest)
        assert all(chunks[n][0] < known for n in passed)
        cube_part(0, 0, cols, first=True)
        for dx in (-1, 1, 2):
            cube_part(dx, 0, known)
        for n in rest:
            relay_chunk(n)
        cube_part(-1, known, cols - known)
        cube_part(1, known, cols - known)
        for n in rest:
            far_chunk(n)
        cube_part(2, known, cols - known)
        result = 3.0 * square[...] - 2.0 * (mask[...] * total[...])
        out_ref[...] = result
        current[...] = result.astype(jnp.bfloat16)

        sent = band.at[s, pl.ds(0, half - rows), :]
        pltpu.make_async_copy(sent, sent, band_send.at[s]).wait()
        shared = band.at[s, pl.ds(0, half), :]
        pltpu.make_async_copy(shared, shared, pair_send.at[s]).wait()
        for which in (0, 1):
            ref = left.at[s, which, :, pl.ds(0, 3 * cols)]
            pltpu.make_async_copy(ref, ref, left_send.at[s, which]).wait()
        return carry

    lax.fori_loop(0, STEPS, step, 0)


def solution(mesh):
    nx, ny, nz = mesh.shape["col"], mesh.shape["row"] // 2, mesh.shape["layer"]

    def shards(hamiltonian, tile_pattern, n_occ, mu, gamma):
        rows, cols = hamiltonian.shape
        order = nx * cols
        chunks = [(n * CHUNK, CHUNK, first) for n, first in CHUNKS]
        ops, count = gather_schedule(ny, nz, rows, chunks)
        vmem = pl.BlockSpec(memory_space=pltpu.VMEM)
        smem = pl.BlockSpec(memory_space=pltpu.SMEM)
        return pl.pallas_call(
            functools.partial(kernel, (nx, ny, nz, rows, cols), chunks, ops),
            out_shape=jax.ShapeDtypeStruct((rows, cols), jnp.float32),
            in_specs=[vmem, vmem, smem, smem, smem],
            out_specs=vmem,
            scratch_shapes=[
                pltpu.VMEM((STEPS, order, cols), jnp.bfloat16),
                pltpu.VMEM((STEPS, 2, rows, order), jnp.bfloat16),
                pltpu.VMEM((rows, cols), jnp.float32),
                pltpu.VMEM((rows, cols), jnp.float32),
                pltpu.VMEM((rows, cols), jnp.float32),
                pltpu.VMEM((rows, cols), jnp.bfloat16),
                pltpu.SemaphoreType.DMA((STEPS, count)),
                pltpu.SemaphoreType.DMA((STEPS,)),
                pltpu.SemaphoreType.DMA((STEPS, len(chunks))),
                pltpu.SemaphoreType.DMA((STEPS,)),
                pltpu.SemaphoreType.DMA((STEPS, 2, 4 * len(chunks))),
                pltpu.SemaphoreType.DMA((STEPS, 2)),
            ],
            compiler_params=pltpu.CompilerParams(
                collective_id=0, has_side_effects=True, vmem_limit_bytes=48 * 2**20),
            name="purify",
        )(hamiltonian, tile_pattern, n_occ, mu, gamma)

    placed = (P(("row", "layer"), "col"), P(), P(), P(), P())
    return jax.shard_map(
        shards, mesh=mesh, in_specs=placed, out_specs=P(("row", "layer"), "col"), check_vma=False
    )
```

time: 121 us -> 117 us (0.967)
  Pallas kernels: 116 us -> 112 us
    pallas_call x1, Pallas kernels: 116 us -> 112 us  [shards(): pl.pallas_call(functools.partial(kernel, (nx, ny, nz, rows, cols), chunks...]
where the time goes in v2:
time: 117 us
  Pallas kernels  112 us (96%)
  local copies, waits for them, and re-layouts  2.4 us (2%)
  between operations  1.96 us (2%)
    pallas_call x1, Pallas kernels, shards(): pl.pallas_call(functools.partial(kernel, (nx, ny, nz, rows, cols), chunks...  112 us
    unnamed x5, local copies, waits for them, and re-layouts  2.4 us

profile of v2, /device:TPU:1, one launch (start us, length us, event | category | flops | bytes accessed | tf_op | source)
XLA Modules:
  0.0 116.6 jit_solution(6777489428988845319)
XLA Ops:
  1.9 0.0 copy-start
  2.0 0.9 copy-done
  2.9 0.0 copy-start.1
  2.9 0.7 copy-done.1
  3.6 112.3 %purify.1 = f32[80,1280]{1,0:T(8,128)S(1)} custom-call(bf16[80,1280]{1,0:T(8,128)(2,1)S(1)} %copy-done, s32[40,40]{1,0:T(8,128)S(1)} %copy-done.1, s32[1]{0:T(128)S(6)} %copy.7.occ_ref, f32[1]{0:T(128)S(6)} %copy.8.mu_ref, f32[1]{0:T(128)S(6)} %copy.9.gamma_ref), custom_call_target="tpu_custom_call" | custom-call | tf_op jit(solution)/shard_map/purify/pallas_call | solution.py:265
  115.9 0.8 copy.10
Async XLA Ops:
  1.9 0.9 copy-start
  2.9 0.7 copy-start.1

commit v3 on v2

--- a/solution.py
+++ b/solution.py
@@ -13,15 +13,17 @@
 STEPS = 2
 MESH = pl.DeviceIdType.MESH
 CHUNK = 256
-CHUNKS = ((0, "y"), (1, "z"), (3, "y"), (2, "z"), (4, "z"))
-
-
-def gather_schedule(ny, nz, rows, chunks, rate=46.65, lat=1.9, ahead=0.8, partner=1.5, late=3.1, product=0.7, hop=3.0):
+CHUNKS = ((0, 2, "y"), (2, 2, "y"), (4, 2, "z"), (6, 2, "z"), (8, 1, "z"), (9, 1, "z"))
+
+
+def gather_schedule(ny, nz, rows, chunks, rate=46.65, lat=2.3, ahead=1.2, partner=1.5, late=5.1, hop=4.5,
+                    issue=0.035, product=0.22):
     ring = {"y": ny, "z": nz}
-    free, events, ops, waiting = {}, [], [], {}
+    free, events, ops, waiting, tasks = {}, [], [], {}, []
     missing = {(n, dy): (nz - (dy == 0)) * c[1] for n, c in enumerate(chunks) for dy in range(ny)}
-    blocks = [0] * len(chunks)
+    parts = [0] * len(chunks)
     count = 0
+    clock = 0.0
 
     def later(t, *event):
         heapq.heappush(events, (t, len(ops), len(events), *event))
@@ -40,14 +42,15 @@
         second = axis != chunks[n][2]
         waiting.setdefault((axis, sign), []).append(((n + late * second, second, hops), piece, hops))
 
-    def pump(t):
-        nonlocal count
+    def pump():
+        nonlocal count, clock
         for (axis, sign), queue in waiting.items():
-            while queue and free.get((axis, sign), 0.0) - ahead <= t:
+            while queue and free.get((axis, sign), 0.0) - ahead <= clock:
                 queue.sort(key=lambda entry: entry[0])
                 _, piece, hops = queue.pop(0)
                 n, dy, dz, c0, w = piece
-                end = max(t, free.get((axis, sign), 0.0)) + rows * w * 2 / rate / 1000
+                clock += issue
+                end = max(clock, free.get((axis, sign), 0.0)) + rows * w * 2 / rate / 1000
                 free[axis, sign] = end
                 ops.append(("send", axis, sign, piece, count))
                 landed = (n, dy - sign, dz, c0, w) if axis == "y" else (n, dy, dz - sign, c0, w)
@@ -59,13 +62,25 @@
         for axis in "yz":
             for sign in (1, -1):
                 offer(axis, sign, (n, 0, 0, c0, w), 0)
-    pump(0.0)
-    while events:
+    pump()
+    while events or tasks:
+        if tasks and (not events or events[0][0] > clock):
+            n, dy = tasks.pop(0)
+            ops.append(("part", n, dy, parts[n]))
+            parts[n] += 1
+            clock += product * max(chunks[n][1], CHUNK) / CHUNK
+            if parts[n] == ny:
+                ops.append(("finish", n))
+                clock += 0.15
+                later(clock + hop, "relay", n)
+            continue
         t, _, _, kind, *rest = heapq.heappop(events)
+        clock = max(clock, t)
         if kind == "land":
             axis, sign, piece, hops, receive = rest
             n, dy, dz, c0, w = piece
             ops.append(("wait", piece, receive))
+            clock += issue
             offer(axis, sign, piece, hops)
             if axis == chunks[n][2]:
                 for way in (1, -1):
@@ -73,20 +88,28 @@
             missing[n, dy % ny] -= w
             if missing[n, dy % ny] == 0:
                 ops.append(("pair", n, dy % ny))
-                blocks[n] += 1
-                if blocks[n] == ny:
-                    later(t + partner, "square", n)
-        elif kind == "square":
-            ops.append(("square", rest[0]))
-            later(t + product + hop, "relay", rest[0])
+                clock += issue
+                later(clock + partner, "ready", n, dy % ny)
+        elif kind == "ready":
+            tasks.append(tuple(rest))
         elif kind == "relay":
             ops.append(("relay", rest[0]))
-        pump(t)
+        pump()
     return ops, count
 
 
-def kernel(sizes, chunks, ops, h_ref, pattern_ref, occ_ref, mu_ref, gamma_ref, out_ref,
-           band, left, mask, square, total, current, band_recv, band_send, pair_recv, pair_send, left_recv, left_send):
+def spans(chunks):
+    merged = []
+    for c0, w, _ in sorted(chunks):
+        if merged and sum(merged[-1]) == c0:
+            merged[-1] = (merged[-1][0], merged[-1][1] + w)
+        else:
+            merged.append((c0, w))
+    return merged
+
+
+def kernel(sizes, chunks, ops, h_hbm, pattern_hbm, occ_ref, mu_ref, gamma_ref, out_ref,
+           h_ref, pattern_ref, band, left, mask, square, total, current, band_recv, band_send, pair_recv, pair_send, left_recv, left_send, in_sem):
     nx, ny, nz, rows, cols = sizes
     order = nx * cols
     half = ny * nz * rows
@@ -101,6 +124,10 @@
     row0 = pl.multiple_of((row * nz + z) * rows, 16)
     col0 = pl.multiple_of(x * cols, 128)
 
+    h_copy = pltpu.make_async_copy(h_hbm, h_ref, in_sem.at[0])
+    pattern_copy = pltpu.make_async_copy(pattern_hbm, pattern_ref, in_sem.at[1])
+    pattern_copy.start()
+    h_copy.start()
     barrier = pltpu.get_barrier_semaphore()
     friends = [partner, *to.values()]
     for friend in friends:
@@ -111,12 +138,14 @@
     row_hot = (row_tile == lax.broadcasted_iota(jnp.int32, (rows, tiles), 1)).astype(jnp.bfloat16)
     col_tile = (col0 + lax.broadcasted_iota(jnp.int32, (tiles, cols), 1)) // TILE
     col_hot = (col_tile == lax.broadcasted_iota(jnp.int32, (tiles, cols), 0)).astype(jnp.bfloat16)
+    pattern_copy.wait()
     picked = jnp.dot(row_hot, pattern_ref[...].astype(jnp.float32).astype(jnp.bfloat16),
                      preferred_element_type=jnp.float32)
     mask[...] = jnp.dot(picked.astype(jnp.bfloat16), col_hot, preferred_element_type=jnp.float32)
     identity = (row0 + lax.broadcasted_iota(jnp.int32, (rows, cols), 0)
                 == col0 + lax.broadcasted_iota(jnp.int32, (rows, cols), 1)).astype(jnp.float32)
     filling = occ_ref[0].astype(jnp.float32) / order
+    h_copy.wait()
     start = mask[...] * (filling * identity + gamma_ref[0] * (mu_ref[0] * identity - h_ref[...].astype(jnp.float32)))
     current[...] = start.astype(jnp.bfloat16)
 
@@ -135,7 +164,7 @@
             begin = pl.multiple_of((2 * ((y + dy) % ny) + core) * nz * rows, 16)
             ref = band.at[s, pl.ds(begin, nz * rows), pl.ds(*chunks[n][:2])]
             return pltpu.make_async_remote_copy(
-                src_ref=ref, dst_ref=ref, send_sem=pair_send.at[s], recv_sem=pair_recv.at[s, n],
+                src_ref=ref, dst_ref=ref, send_sem=pair_send.at[s], recv_sem=pair_recv.at[s, ny * n + dy],
                 device_id=partner, device_id_type=MESH)
 
         def along_x(which, sign, dx, c0, w, receive):
@@ -164,42 +193,60 @@
             along_x(0, 1, -2, 0, mid, 2).wait_recv()
             along_x(0, -1, -2, mid, mid, 3).wait_recv()
 
-        def square_chunk(n):
-            c0, w, _ = chunks[n]
-            arrived = band.at[s, pl.ds(0, half), pl.ds(c0, w)]
-            pltpu.make_async_copy(arrived, arrived, pair_recv.at[s, n]).wait()
-            product = jnp.dot(left[s, 0], band[s, :, c0:c0 + w], preferred_element_type=jnp.float32)
-            product = mask[:, c0:c0 + w] * product
-            square[:, c0:c0 + w] = product
-            left[s, 1, :, pl.ds(pl.multiple_of(col0 + c0, 128), w)] = product.astype(jnp.bfloat16)
+        def square_part(n, dy, turn):
+            c0, w, _ = chunks[n]
+            arrived = band.at[s, pl.ds(0, nz * rows), pl.ds(c0, w)]
+            pltpu.make_async_copy(arrived, arrived, pair_recv.at[s, ny * n + dy]).wait()
+            deep = 2 * nz * rows
+            at = pl.multiple_of(((y + dy) % ny) * deep, 128)
+            product = jnp.dot(left[s, 0, :, pl.ds(at, deep)], band[s, pl.ds(at, deep), c0:c0 + w],
+                              preferred_element_type=jnp.float32)
+            if turn == 0:
+                square[:, c0:c0 + w] = product
+            elif turn < ny - 1:
+                square[:, c0:c0 + w] += product
+            else:
+                product = mask[:, c0:c0 + w] * (square[:, c0:c0 + w] + product)
+                square[:, c0:c0 + w] = product
+                left[s, 1, :, pl.ds(pl.multiple_of(col0 + c0, 128), w)] = product.astype(jnp.bfloat16)
+
+        def square_send(n):
+            c0, w, _ = chunks[n]
             along_x(1, 1, 0, c0, w, 4 * n).start()
             along_x(1, -1, 0, c0, w, 4 * n + 1).start()
 
+        def far_parts(n):
+            c0, w, _ = chunks[n]
+            cut = (w // 2 + LANES * (1 - c0 // LANES % 2) // 2) // LANES * LANES
+            return [part for part in ((1, c0, cut, 4 * n + 2), (-1, c0 + cut, w - cut, 4 * n + 3)) if part[2]]
+
         def relay_chunk(n):
             c0, w, _ = chunks[n]
-            cut = w // 2
-            along_x(1, 1, -1, c0, w, 4 * n).wait_recv()
-            along_x(1, 1, -1, c0, cut, 4 * n + 2).start()
-            along_x(1, -1, 1, c0, w, 4 * n + 1).wait_recv()
-            along_x(1, -1, 1, c0 + cut, w - cut, 4 * n + 3).start()
+            for sign, begin, width, receive in far_parts(n):
+                along_x(1, sign, -sign, c0, w, receive - 2).wait_recv()
+                along_x(1, sign, -sign, begin, width, receive).start()
+
+        def near_chunk(n):
+            c0, w, _ = chunks[n]
+            for sign in {1, -1} - {part[0] for part in far_parts(n)}:
+                along_x(1, sign, -sign, c0, w, 4 * n + (0 if sign > 0 else 1)).wait_recv()
 
         def far_chunk(n):
-            c0, w, _ = chunks[n]
-            cut = w // 2
-            along_x(1, 1, -2, c0, cut, 4 * n + 2).wait_recv()
-            along_x(1, -1, -2, c0 + cut, w - cut, 4 * n + 3).wait_recv()
-
-        def cube_part(dx, k0, width, first=False):
-            at = pl.multiple_of(((x + dx + nx) % nx) * cols + k0, 128)
-            for c0, w, _ in chunks:
-                part = jnp.dot(left[s, 1, :, pl.ds(at, width)], band[s, pl.ds(at, width), c0:c0 + w],
-                               preferred_element_type=jnp.float32)
-                if first:
-                    total[:, c0:c0 + w] = part
-                else:
-                    total[:, c0:c0 + w] += part
-
-        begun, relayed, squared, passed = False, False, [], []
+            for sign, begin, width, receive in far_parts(n):
+                along_x(1, sign, -2, begin, width, receive).wait_recv()
+
+        def cube_part(dx, ranges, first=False):
+            for k0, width in ranges:
+                at = pl.multiple_of(((x + dx + nx) % nx) * cols + k0, 128)
+                for c0 in range(0, cols, CHUNK):
+                    part = jnp.dot(left[s, 1, :, pl.ds(at, width)], band[s, pl.ds(at, width), c0:c0 + CHUNK],
+                                   preferred_element_type=jnp.float32)
+                    if first:
+                        total[:, c0:c0 + CHUNK] = part
+                    else:
+                        total[:, c0:c0 + CHUNK] += part
+
+        begun, relayed, started, done, passed = False, False, False, [], []
         for op in ops:
             if op[0] == "send":
                 along(*op[1:]).start()
@@ -208,34 +255,40 @@
                     begun = True
                     left_begin()
                 along("y", 1, *op[1:]).wait_recv()
-                if not relayed and op[2] > 40:
+                if not relayed and op[2] > 60:
                     relayed = True
                     left_relay()
             elif op[0] == "pair":
                 to_partner(*op[1:]).start()
-            elif op[0] == "square":
-                if not squared:
+            elif op[0] == "part":
+                if not started:
+                    started = True
                     left_end()
-                square_chunk(op[1])
-                squared.append(op[1])
-            elif len(squared) < len(chunks):
+                square_part(*op[1:])
+            elif op[0] == "finish":
+                square_send(op[1])
+                done.append(op[1])
+            elif len(done) < len(chunks):
                 relay_chunk(op[1])
                 passed.append(op[1])
+        rest = [n for n in done if n not in passed]
+        early, late = spans([chunks[n] for n in passed]), spans([chunks[n] for n in rest])
+        cube_part(0, [(0, cols)], first=True)
+        relay_chunk(rest[0])
         for n in passed:
+            near_chunk(n)
             far_chunk(n)
-        rest = [n for n in squared if n not in passed]
-        known = min(chunks[n][0] for n in rest)
-        assert all(chunks[n][0] < known for n in passed)
-        cube_part(0, 0, cols, first=True)
         for dx in (-1, 1, 2):
-            cube_part(dx, 0, known)
+            cube_part(dx, early)
+        for n in rest[1:]:
+            relay_chunk(n)
         for n in rest:
-            relay_chunk(n)
-        cube_part(-1, known, cols - known)
-        cube_part(1, known, cols - known)
+            near_chunk(n)
+        cube_part(-1, late)
+        cube_part(1, late)
         for n in rest:
             far_chunk(n)
-        cube_part(2, known, cols - known)
+        cube_part(2, late)
         result = 3.0 * square[...] - 2.0 * (mask[...] * total[...])
         out_ref[...] = result
         current[...] = result.astype(jnp.bfloat16)
@@ -258,16 +311,19 @@
     def shards(hamiltonian, tile_pattern, n_occ, mu, gamma):
         rows, cols = hamiltonian.shape
         order = nx * cols
-        chunks = [(n * CHUNK, CHUNK, first) for n, first in CHUNKS]
+        chunks = [(n * LANES, w * LANES, first) for n, w, first in CHUNKS]
         ops, count = gather_schedule(ny, nz, rows, chunks)
+        hbm = pl.BlockSpec(memory_space=pltpu.HBM)
         vmem = pl.BlockSpec(memory_space=pltpu.VMEM)
         smem = pl.BlockSpec(memory_space=pltpu.SMEM)
         return pl.pallas_call(
             functools.partial(kernel, (nx, ny, nz, rows, cols), chunks, ops),
             out_shape=jax.ShapeDtypeStruct((rows, cols), jnp.float32),
-            in_specs=[vmem, vmem, smem, smem, smem],
+            in_specs=[hbm, hbm, smem, smem, smem],
             out_specs=vmem,
             scratch_shapes=[
+                pltpu.VMEM((rows, cols), jnp.bfloat16),
+                pltpu.VMEM(tile_pattern.shape, jnp.int32),
                 pltpu.VMEM((STEPS, order, cols), jnp.bfloat16),
                 pltpu.VMEM((STEPS, 2, rows, order), jnp.bfloat16),
                 pltpu.VMEM((rows, cols), jnp.float32),
@@ -276,10 +332,11 @@
                 pltpu.VMEM((rows, cols), jnp.bfloat16),
                 pltpu.SemaphoreType.DMA((STEPS, count)),
                 pltpu.SemaphoreType.DMA((STEPS,)),
-                pltpu.SemaphoreType.DMA((STEPS, len(chunks))),
+                pltpu.SemaphoreType.DMA((STEPS, ny * len(chunks))),
                 pltpu.SemaphoreType.DMA((STEPS,)),
                 pltpu.SemaphoreType.DMA((STEPS, 2, 4 * len(chunks))),
                 pltpu.SemaphoreType.DMA((STEPS, 2)),
+                pltpu.SemaphoreType.DMA((2,)),
             ],
             compiler_params=pltpu.CompilerParams(
                 collective_id=0, has_side_effects=True, vmem_limit_bytes=48 * 2**20),

time: 117 us -> 113 us (0.966)
  Pallas kernels: 112 us -> 108 us
    pallas_call x1, Pallas kernels: 112 us -> 108 us  [shards(): pl.pallas_call(functools.partial(kernel, (nx, ny, nz, rows, cols), chunks...]
where the time goes in v3:
time: 113 us; the launch traced here: 112 us
  Pallas kernels  108 us (96%)
  local copies, waits for them, and re-layouts  2.4 us (2%)
  between operations  1.96 us (2%)
    pallas_call x1, Pallas kernels, shards(): pl.pallas_call(functools.partial(kernel, (nx, ny, nz, rows, cols), chunks...  108 us
    unnamed x5, local copies, waits for them, and re-layouts  2.4 us

profile of v3, /device:TPU:1, one launch (start us, length us, event | category | flops | bytes accessed | tf_op | source)
XLA Modules:
  0.0 112.5 jit_solution(8665935338284667219)
XLA Ops:
  1.9 0.0 copy-start
  2.0 0.9 copy-done
  2.9 0.0 copy-start.1
  2.9 0.7 copy-done.1
  3.6 108.1 %purify.1 = f32[80,1280]{1,0:T(8,128)S(1)} custom-call(bf16[80,1280]{1,0:T(8,128)(2,1)S(1)} %copy-done, s32[40,40]{1,0:T(8,128)S(1)} %copy-done.1, s32[1]{0:T(128)S(6)} %copy.7.occ_ref, f32[1]{0:T(128)S(6)} %copy.8.mu_ref, f32[1]{0:T(128)S(6)} %copy.9.gamma_ref), custom_call_target="tpu_custom_call" | custom-call | tf_op jit(solution)/shard_map/purify/pallas_call | solution.py:319
  111.7 0.8 copy.10
Async XLA Ops:
  1.9 0.9 copy-start
  2.9 0.7 copy-start.1

commit v4 on v3

--- a/solution.py
+++ b/solution.py
@@ -13,7 +13,7 @@
 STEPS = 2
 MESH = pl.DeviceIdType.MESH
 CHUNK = 256
-CHUNKS = ((0, 2, "y"), (2, 2, "y"), (4, 2, "z"), (6, 2, "z"), (8, 1, "z"), (9, 1, "z"))
+CHUNKS = ((0, 1, "y"), (1, 2, "y"), (3, 2, "z"), (5, 2, "z"), (7, 2, "z"), (9, 1, "y"))
 
 
 def gather_schedule(ny, nz, rows, chunks, rate=46.65, lat=2.3, ahead=1.2, partner=1.5, late=5.1, hop=4.5,
@@ -108,8 +108,8 @@
     return merged
 
 
-def kernel(sizes, chunks, ops, h_hbm, pattern_hbm, occ_ref, mu_ref, gamma_ref, out_ref,
-           h_ref, pattern_ref, band, left, mask, square, total, current, band_recv, band_send, pair_recv, pair_send, left_recv, left_send, in_sem):
+def kernel(sizes, chunks, ops, h_hbm, pattern_hbm, occ_hbm, mu_hbm, gamma_hbm, out_ref,
+           h_ref, pattern_ref, occ_ref, mu_ref, gamma_ref, band, left, mask, square, total, current, band_recv, band_send, pair_recv, pair_send, left_recv, left_send, in_sem):
     nx, ny, nz, rows, cols = sizes
     order = nx * cols
     half = ny * nz * rows
@@ -126,8 +126,10 @@
 
     h_copy = pltpu.make_async_copy(h_hbm, h_ref, in_sem.at[0])
     pattern_copy = pltpu.make_async_copy(pattern_hbm, pattern_ref, in_sem.at[1])
-    pattern_copy.start()
-    h_copy.start()
+    scalar_copies = [pltpu.make_async_copy(hbm, ref, in_sem.at[2 + i]) for i, (hbm, ref) in enumerate(
+        ((occ_hbm, occ_ref), (mu_hbm, mu_ref), (gamma_hbm, gamma_ref)))]
+    for copy in (pattern_copy, h_copy, *scalar_copies):
+        copy.start()
     barrier = pltpu.get_barrier_semaphore()
     friends = [partner, *to.values()]
     for friend in friends:
@@ -144,6 +146,8 @@
     mask[...] = jnp.dot(picked.astype(jnp.bfloat16), col_hot, preferred_element_type=jnp.float32)
     identity = (row0 + lax.broadcasted_iota(jnp.int32, (rows, cols), 0)
                 == col0 + lax.broadcasted_iota(jnp.int32, (rows, cols), 1)).astype(jnp.float32)
+    for copy in scalar_copies:
+        copy.wait()
     filling = occ_ref[0].astype(jnp.float32) / order
     h_copy.wait()
     start = mask[...] * (filling * identity + gamma_ref[0] * (mu_ref[0] * identity - h_ref[...].astype(jnp.float32)))
@@ -315,15 +319,17 @@
         ops, count = gather_schedule(ny, nz, rows, chunks)
         hbm = pl.BlockSpec(memory_space=pltpu.HBM)
         vmem = pl.BlockSpec(memory_space=pltpu.VMEM)
-        smem = pl.BlockSpec(memory_space=pltpu.SMEM)
         return pl.pallas_call(
             functools.partial(kernel, (nx, ny, nz, rows, cols), chunks, ops),
             out_shape=jax.ShapeDtypeStruct((rows, cols), jnp.float32),
-            in_specs=[hbm, hbm, smem, smem, smem],
+            in_specs=[hbm] * 5,
             out_specs=vmem,
             scratch_shapes=[
                 pltpu.VMEM((rows, cols), jnp.bfloat16),
                 pltpu.VMEM(tile_pattern.shape, jnp.int32),
+                pltpu.SMEM((1,), jnp.int32),
+                pltpu.SMEM((1,), jnp.float32),
+                pltpu.SMEM((1,), jnp.float32),
                 pltpu.VMEM((STEPS, order, cols), jnp.bfloat16),
                 pltpu.VMEM((STEPS, 2, rows, order), jnp.bfloat16),
                 pltpu.VMEM((rows, cols), jnp.float32),
@@ -336,12 +342,12 @@
                 pltpu.SemaphoreType.DMA((STEPS,)),
                 pltpu.SemaphoreType.DMA((STEPS, 2, 4 * len(chunks))),
                 pltpu.SemaphoreType.DMA((STEPS, 2)),
-                pltpu.SemaphoreType.DMA((2,)),
+                pltpu.SemaphoreType.DMA((5,)),
             ],
             compiler_params=pltpu.CompilerParams(
                 collective_id=0, has_side_effects=True, vmem_limit_bytes=48 * 2**20),
             name="purify",
-        )(hamiltonian, tile_pattern, n_occ, mu, gamma)
+        )(*(pltpu.with_memory_space_constraint(v, pltpu.HBM) for v in (hamiltonian, tile_pattern)), n_occ, mu, gamma)
 
     placed = (P(("row", "layer"), "col"), P(), P(), P(), P())
     return jax.shard_map(

time: 113 us -> 110 us (0.973)
  local copies, waits for them, and re-layouts: 2.4 us -> 0.75 us
    unnamed x5 -> x1, local copies, waits for them, and re-layouts: 2.4 us -> 0.75 us
where the time goes in v4:
time: 110 us
  Pallas kernels  107 us (97%)
  between operations  1.95 us (2%)
    pallas_call x1, Pallas kernels, shards(): pl.pallas_call(functools.partial(kernel, (nx, ny, nz, rows, cols), chunks...  107 us

profile of v4, /device:TPU:1, one launch (start us, length us, event | category | flops | bytes accessed | tf_op | source)
XLA Modules:
  0.0 109.8 jit_solution(32845000761357590)
XLA Ops:
  1.9 107.1 %purify.1 = f32[80,1280]{1,0:T(8,128)S(1)} custom-call(bf16[80,1280]{1,0:T(8,128)(2,1)} %h_hbm.1, s32[40,40]{1,0:T(8,128)} %pattern_hbm.1, s32[1]{0:T(128)S(6)} %copy.7.occ_hbm, f32[1]{0:T(128)S(6)} %copy.8.mu_hbm, f32[1]{0:T(128)S(6)} %copy.9.gamma_hbm), custom_call_target="tpu_custom_call" | custom-call | tf_op jit(solution)/shard_map/purify/pallas_call | solution.py:322
  109.1 0.8 copy.10

commit v5 on v4

--- a/solution.py
+++ b/solution.py
@@ -13,11 +13,11 @@
 STEPS = 2
 MESH = pl.DeviceIdType.MESH
 CHUNK = 256
-CHUNKS = ((0, 1, "y"), (1, 2, "y"), (3, 2, "z"), (5, 2, "z"), (7, 2, "z"), (9, 1, "y"))
-
-
-def gather_schedule(ny, nz, rows, chunks, rate=46.65, lat=2.3, ahead=1.2, partner=1.5, late=5.1, hop=4.5,
-                    issue=0.035, product=0.22):
+CHUNKS = ((0, 2, "y"), (2, 1, "y"), (3, 2, "z"), (5, 2, "z"), (7, 2, "z"), (9, 1, "y"))
+
+
+def gather_schedule(ny, nz, rows, chunks, rate=46.65, lat=2.3, ahead=1.45, partner=1.5, late=5.1, hop=4.5,
+                    issue=0.035, product=0.3):
     ring = {"y": ny, "z": nz}
     free, events, ops, waiting, tasks = {}, [], [], {}, []
     missing = {(n, dy): (nz - (dy == 0)) * c[1] for n, c in enumerate(chunks) for dy in range(ny)}

time: 110 us -> 109 us (level)
  no operation moved by 1% of the time
where the time goes in v5:
time: 109 us
  Pallas kernels  106 us (97%)
  between operations  1.95 us (2%)
    pallas_call x1, Pallas kernels, shards(): pl.pallas_call(functools.partial(kernel, (nx, ny, nz, rows, cols), chunks...  106 us

profile of v5, /device:TPU:1, one launch (start us, length us, event | category | flops | bytes accessed | tf_op | source)
XLA Modules:
  0.0 109.0 jit_solution(10706721315735879910)
XLA Ops:
  1.9 106.3 %purify.1 = f32[80,1280]{1,0:T(8,128)S(1)} custom-call(bf16[80,1280]{1,0:T(8,128)(2,1)} %h_hbm.1, s32[40,40]{1,0:T(8,128)} %pattern_hbm.1, s32[1]{0:T(128)S(6)} %copy.7.occ_hbm, f32[1]{0:T(128)S(6)} %copy.8.mu_hbm, f32[1]{0:T(128)S(6)} %copy.9.gamma_hbm), custom_call_target="tpu_custom_call" | custom-call | tf_op jit(solution)/shard_map/purify/pallas_call | solution.py:322
  108.3 0.8 copy.10
